TPU v7x, 1024 devices: a whole 4x8x16 slice. The times are simulated.
1024 devices in a mesh: grp: 16 (over y, x_lo), pme: 64 (over x_hi, z, core).
Axes of the slice: x: 4 (x_hi: 2, x_lo: 2; x = x_hi * 2 + x_lo), y: 8, z: 16, core: 2. Of those that a mesh axis runs over, the one named last changes fastest.
Arguments:
- charge: float32 [131072], P(('grp', 'pme')), may hold values from -4 to 4
- base: int32 [3, 131072], P(None, ('grp', 'pme')), may hold values from 0 to 255, as said below
- frac: float32 [3, 131072], P(None, ('grp', 'pme')), may hold values from 0 to 1
- counts: int32 [1024], P(('grp', 'pme')), may hold values from 16 to 128, as said below
- green: float32 [128, 256, 512], P('grp', 'pme'), may hold values from 0.05 to 0.5
Outputs:
- field: float32 [4, 131072], P(None, ('grp', 'pme'))
Inputs may be any that keep to these rules, and one draw needn't show every extreme that they name: `base`: row 0 holds an atom's first mesh index along x (below 256), row 1 along y (below 256), row 2 the first of its four planes counted from the first plane of its slab (below 8). Block d's live atoms are its first counts[d] slots; other slots hold data that is ignored. Some block is full in every draw.
All inputs are finite; a program needn't handle non-finite values.
Results may differ from a plain program's by a relative error of at most 0.007.
Values may be sent and summed in bfloat16 or wider, within the bound.
No kernel may reach another device: no remote copies, remote signals or barrier semaphores. Data moves between devices by JAX's collectives and lax.ppermute only.
A program may use at most 32 MiB of HBM per device.

v0:
```python
import functools
import math

import jax
import jax.numpy as jnp
import numpy as np
from jax import lax
from jax.experimental import pallas as pl
from jax.experimental.pallas import tpu as pltpu
from jax.sharding import PartitionSpec as P

NX = 256
NY = 256
NZ = 512
SLABS = 64
GROUPS = 16
KX = 8
KY = 4
CZ = NZ // SLABS
PLANES = CZ + 3
ATOMS = 128
LANES = 128
TWO_PI = 2.0 * math.pi

f32 = jnp.float32
bf16 = jnp.bfloat16
VMEM = pl.BlockSpec(memory_space=pltpu.VMEM)


@functools.cache
def y_table():
    wave = np.arange(NY).reshape(SLABS, 1, KY, 1)
    angle = (wave * np.arange(NY).reshape(1, 1, 1, NY) % NY) * (TWO_PI / NY)
    cosine, sine = np.cos(angle), np.sin(angle)
    real = np.stack([cosine, sine], axis=3)
    imag = np.stack([-sine, cosine], axis=3)
    return np.concatenate([real, imag], axis=1).reshape(NY * 2, NY * 2).astype(jnp.bfloat16)


@functools.cache
def slab_table():
    angle = (np.arange(SLABS)[:, None] * np.arange(128)[None, :] % SLABS) * (TWO_PI / SLABS)
    cosine, sine = np.cos(angle), np.sin(angle)
    table = np.concatenate(
        [np.concatenate([cosine, -sine], axis=1), np.concatenate([sine, cosine], axis=1)], axis=0
    )
    return table.astype(jnp.bfloat16)


@functools.cache
def plane_table():
    angle = (np.arange(16)[:, None] * np.arange(NZ)[None, :] % NZ) * (TWO_PI / NZ)
    return np.cos(angle).astype(np.float32), np.sin(angle).astype(np.float32)


def spline(u):
    other = 1.0 - u
    square = u * u
    cube = square * u
    return (
        other * other * other * (1.0 / 6.0),
        (3.0 * cube - 6.0 * square + 4.0) * (1.0 / 6.0),
        (-3.0 * cube + 3.0 * square + 3.0 * u + 1.0) * (1.0 / 6.0),
        cube * (1.0 / 6.0),
    )


def spline_slopes(u):
    other = 1.0 - u
    square = u * u
    return (
        other * other * -0.5,
        (3.0 * square - 4.0 * u) * 0.5,
        (-3.0 * square + 2.0 * u + 1.0) * 0.5,
        square * 0.5,
    )


def unit_circle(turns):
    quarter = (turns + 32) >> 6
    x = (turns - (quarter << 6)).astype(f32) * (TWO_PI / 256)
    x2 = x * x
    s = x * (1.0 + x2 * (-1.0 / 6 + x2 * (1.0 / 120 + x2 * (-1.0 / 5040 + x2 * (1.0 / 362880)))))
    c = 1.0 + x2 * (-0.5 + x2 * (1.0 / 24 + x2 * (-1.0 / 720 + x2 * (1.0 / 40320))))
    odd = (quarter & 1) == 1
    cosine = jnp.where(odd, s, c)
    sine = jnp.where(odd, c, s)
    cosine = jnp.where(((quarter + 1) & 2) == 2, -cosine, cosine)
    sine = jnp.where((quarter & 2) == 2, -sine, sine)
    return cosine, sine


def dot(a, b, dims=((1,), (0,))):
    return lax.dot_general(a, b, (dims, ((), ())), preferred_element_type=f32)


def row(values, k):
    return values[k : k + 1, :]


def x_steps(kx):
    return [unit_circle((kx * j) & (NX - 1)) for j in range(1, 4)]


def x_terms(weights, g, steps):
    even = row(weights[0], g)
    odd = 0.0
    for j in range(1, 4):
        w = row(weights[j], g)
        even = even + w * steps[j - 1][0]
        odd = odd + w * steps[j - 1][1]
    return even, odd


def turned(start, terms):
    cosine, sine = start
    even, odd = terms
    return cosine * even - sine * odd, -(sine * even + cosine * odd)


def placed(rel, weights, g):
    out = jnp.zeros(rel.shape, f32)
    for j in range(4):
        out = jnp.where(rel == j, row(weights[j], g), out)
    return out


def kernel_pack(count_hbm, charge_hbm, frac_hbm, base_hbm, out_ref, factor_ref, count_ref, charge_ref, frac_ref, base_ref, sems):
    moves = ((count_hbm, count_ref), (charge_hbm, charge_ref), (frac_hbm, frac_ref), (base_hbm, base_ref))
    copies = [pltpu.make_async_copy(a, b, sems.at[i]) for i, (a, b) in enumerate(moves)]
    for copy in copies:
        copy.start()
    for copy in copies:
        copy.wait()
    live = lax.broadcasted_iota(jnp.int32, (1, ATOMS), 1) < count_ref[0]
    loaded = jnp.where(live, charge_ref[...], 0.0)
    rows = [loaded, frac_ref[...], base_ref[...].astype(f32)]
    for g in range(GROUPS):
        out_ref[g] = jnp.concatenate(rows + [jnp.full((1, ATOMS), float(g), f32)], axis=0)
    factor_ref[...] = jnp.concatenate([jnp.where(live, 1.0, 0.0), loaded, loaded, loaded], axis=0)


def whole(values):
    return values.astype(jnp.int32)


def own_waves(atoms_ref):
    return whole(atoms_ref[0, 7:8, :]) * KX + lax.broadcasted_iota(jnp.int32, (KX, ATOMS), 0)


def kernel_spread(atoms_ref, table_ref, out_ref, y_ref, lead_ref):
    kx = own_waves(atoms_ref)
    steps = x_steps(kx)
    charge = atoms_ref[:, 0, :]
    wx, wy, wz = (spline(atoms_ref[:, 1 + d, :]) for d in range(3))
    bx, by, bz = (whole(atoms_ref[:, 4 + d, :]) for d in range(3))
    y_at = lax.broadcasted_iota(jnp.int32, (NY, ATOMS), 0)
    z_at = lax.broadcasted_iota(jnp.int32, (16, ATOMS), 0)
    wz = [charge * w for w in wz]
    blank = jnp.zeros((LANES - PLANES * KX, ATOMS), f32)
    for g in range(GROUPS):
        here = pl.ds(g * ATOMS, ATOMS)
        y_ref[:, here] = placed((y_at - row(by, g)) & (NY - 1), wy, g).astype(bf16)
        start = unit_circle((kx * row(bx, g)) & (NX - 1))
        real, imag = turned(start, x_terms(wx, g, steps))
        z = placed(z_at - row(bz, g), wz, g)
        lead = [row(z, k) * real for k in range(PLANES)] + [blank]
        lead_ref[0:LANES, here] = jnp.concatenate(lead, axis=0).astype(bf16)
        lead = [row(z, k) * imag for k in range(PLANES)] + [blank]
        lead_ref[LANES : 2 * LANES, here] = jnp.concatenate(lead, axis=0).astype(bf16)
    mesh = dot(y_ref[...], lead_ref[...], ((1,), (1,)))
    mesh = jnp.concatenate([mesh[:, :LANES], mesh[:, LANES:]], axis=0)
    waves = dot(table_ref[...], mesh.astype(bf16))
    out_ref[...] = waves.reshape(SLABS, 2 * KY, LANES).astype(bf16)


def kernel_waves(mesh_ref, green_ref, table_ref, cos_ref, sin_ref, out_ref, in_ref, hold_ref):
    in_ref[...] = mesh_ref[...].astype(f32)
    blank = jnp.zeros((LANES - PLANES * KX, 2 * LANES), f32)
    for k in range(KY):
        slabs = jnp.concatenate([in_ref[:, k, :], in_ref[:, KY + k, :]], axis=0).astype(bf16)
        part = dot(slabs, table_ref[...], ((0,), (0,)))
        real = [None] * 4
        imag = [None] * 4
        for z in range(PLANES):
            a = part[z * KX : (z + 1) * KX, :LANES]
            b = part[z * KX : (z + 1) * KX, LANES:]
            for m in range(4):
                if z == 0:
                    real[m], imag[m] = a, b
                    continue
                c = cos_ref[z : z + 1, m * LANES : (m + 1) * LANES]
                s = sin_ref[z : z + 1, m * LANES : (m + 1) * LANES]
                real[m] = real[m] + (a * c + b * s)
                imag[m] = imag[m] + (b * c - a * s)
        for m in range(4):
            factor = green_ref[:, k, m * LANES : (m + 1) * LANES] * (1.0 / (NY * NZ))
            real[m] = real[m] * factor
            imag[m] = imag[m] * factor
        rows = []
        for z in range(PLANES):
            a = b = 0.0
            for m in range(4):
                if z == 0:
                    a, b = a + real[m], b + imag[m]
                    continue
                c = cos_ref[z : z + 1, m * LANES : (m + 1) * LANES]
                s = sin_ref[z : z + 1, m * LANES : (m + 1) * LANES]
                a = a + (real[m] * c - imag[m] * s)
                b = b + (imag[m] * c + real[m] * s)
            rows.append(jnp.concatenate([a, b], axis=1))
        back = jnp.concatenate(rows + [blank], axis=0)
        cells = dot(table_ref[...], back.astype(bf16), ((1,), (1,)))
        hold_ref[:, k, :] = cells[:SLABS]
        hold_ref[:, KY + k, :] = cells[SLABS:]
    out_ref[...] = hold_ref[...].astype(bf16)


def kernel_sample(atoms_ref, mesh_ref, table_ref, out_ref, y_ref):
    kx = own_waves(atoms_ref)
    steps = x_steps(kx)
    wx, wy, wz = (spline(atoms_ref[:, 1 + d, :]) for d in range(3))
    dx, dy, dz = (spline_slopes(atoms_ref[:, 1 + d, :]) for d in range(3))
    bx, by, bz = (whole(atoms_ref[:, 4 + d, :]) for d in range(3))
    y_at = lax.broadcasted_iota(jnp.int32, (NY, ATOMS), 0)
    z_at = lax.broadcasted_iota(jnp.int32, (16, ATOMS), 0)
    waves = mesh_ref[...].reshape(2 * NY, LANES).T
    cells = dot(waves, table_ref[...]).astype(bf16)
    used = PLANES * KX
    cells = jnp.concatenate([cells[:used, :NY], cells[:used, NY:]], axis=0)
    for g in range(GROUPS):
        rel = (y_at - row(by, g)) & (NY - 1)
        y_ref[:, 0:ATOMS] = placed(rel, wy, g).astype(bf16)
        y_ref[:, ATOMS : 2 * ATOMS] = placed(rel, dy, g).astype(bf16)
        values = dot(cells, y_ref[...])
        start = unit_circle((kx * row(bx, g)) & (NX - 1))
        x_real, x_imag = turned(start, x_terms(wx, g, steps))
        s_real, s_imag = turned(start, x_terms(dx, g, steps))
        z = placed(z_at - row(bz, g), wz, g)
        dzt = placed(z_at - row(bz, g), dz, g)
        plain = [0.0, 0.0]
        along_y = [0.0, 0.0]
        along_z = [0.0, 0.0]
        for part in range(2):
            for k in range(PLANES):
                at = part * used + k * KX
                here = values[at : at + KX]
                plain[part] = plain[part] + row(z, k) * here[:, :ATOMS]
                along_y[part] = along_y[part] + row(z, k) * here[:, ATOMS:]
                along_z[part] = along_z[part] + row(dzt, k) * here[:, :ATOMS]
        terms = (
            x_real * plain[0] + x_imag * plain[1],
            s_real * plain[0] + s_imag * plain[1],
            x_real * along_y[0] + x_imag * along_y[1],
            x_real * along_z[0] + x_imag * along_z[1],
        )
        out_ref[g] = jnp.concatenate([jnp.sum(t, axis=0, keepdims=True) for t in terms], axis=0)


def kernel_total(factor_ref, terms_ref, out_ref):
    total = terms_ref[0]
    for g in range(1, GROUPS):
        total = total + terms_ref[g]
    out_ref[...] = total * factor_ref[...]


def call(kernel, shape, dtype, inputs, scratch=(), flops=0, limit=8):
    return pl.pallas_call(
        kernel,
        out_shape=jax.ShapeDtypeStruct(shape, dtype),
        in_specs=[VMEM] * inputs,
        out_specs=VMEM,
        scratch_shapes=scratch,
        name=kernel.__name__,
        compiler_params=pltpu.CompilerParams(vmem_limit_bytes=limit << 20),
        cost_estimate=pl.CostEstimate(flops=flops, bytes_accessed=1 << 20, transcendentals=0),
    )


def pack(counts, charge, frac, base):
    return pl.pallas_call(
        kernel_pack,
        out_shape=[
            jax.ShapeDtypeStruct((GROUPS, 8, ATOMS), f32),
            jax.ShapeDtypeStruct((4, ATOMS), f32),
        ],
        in_specs=[pl.BlockSpec(memory_space=pltpu.HBM)] * 4,
        out_specs=[VMEM, VMEM],
        scratch_shapes=[
            pltpu.SMEM((1,), jnp.int32),
            pltpu.VMEM((1, ATOMS), f32),
            pltpu.VMEM((3, ATOMS), f32),
            pltpu.VMEM((3, ATOMS), jnp.int32),
            pltpu.SemaphoreType.DMA((4,)),
        ],
        name="kernel_pack",
        compiler_params=pltpu.CompilerParams(vmem_limit_bytes=60 << 20),
        cost_estimate=pl.CostEstimate(flops=1 << 30, bytes_accessed=1 << 20, transcendentals=0),
    )(counts, charge, frac, base)


def spread(atoms):
    scratch = [pltpu.VMEM((NY, GROUPS * ATOMS), bf16), pltpu.VMEM((2 * LANES, GROUPS * ATOMS), bf16)]
    run = call(kernel_spread, (SLABS, 2 * KY, LANES), bf16, 2, scratch, 1 << 30)
    return run(atoms, jnp.asarray(y_table()))


def wave_product(mesh, green):
    scratch = [pltpu.VMEM((SLABS, 2 * KY, LANES), f32)] * 2
    run = call(kernel_waves, (SLABS, 2 * KY, LANES), bf16, 5, scratch, 1 << 30)
    return run(mesh, green, jnp.asarray(slab_table()), *map(jnp.asarray, plane_table()))


def sample(atoms, mesh):
    scratch = [pltpu.VMEM((NY, 2 * ATOMS), bf16)]
    run = call(kernel_sample, (GROUPS, 4, ATOMS), f32, 3, scratch, 1 << 30)
    return run(atoms, mesh, jnp.asarray(y_table()))


def total(factors, terms):
    return call(kernel_total, (4, ATOMS), f32, 2)(factors, terms)


def body(charge, base, frac, counts, green):
    charge = charge.reshape(1, ATOMS)
    swap = functools.partial(lax.all_to_all, split_axis=0, concat_axis=0, tiled=True)
    packed, factors = pack(counts, charge, frac, base)
    atoms = swap(packed, "grp")
    mesh = swap(spread(atoms), "pme")
    mesh = swap(wave_product(mesh, green), "pme")
    terms = swap(sample(atoms, mesh), "grp")
    return total(factors, terms)


def solution(mesh):
    both = ("grp", "pme")
    placed_in = (P(both), P(None, both), P(None, both), P(both), P("grp", "pme", None))
    return jax.shard_map(body, mesh=mesh, in_specs=placed_in, out_specs=P(None, both), check_vma=False)
```

profile of v0, /device:TPU:1, one launch (start us, length us, event | category | flops | bytes accessed | tf_op | source)
XLA Modules:
  0.0 99.8 jit_solution(17211100664447311378)
XLA Ops:
  0.7 0.0 copy-start.2
  0.7 1.4 %kernel_pack.1 = (f32[16,8,128]{2,1,0:T(8,128)}, f32[4,128]{1,0:T(4,128)}) custom-call(s32[1]{0:T(128)S(6)} %copy.10.count_hbm, f32[1,128]{1,0:T(1,128)} %bitcast.1, f32[3,128]{1,0:T(4,128)} %frac_hbm.1, s32[3,128]{1,0:T(4,128)} %base_hbm.1), custom_call_target="tpu_custom_call" | custom-call | flops 1073741824 | bytes 1048576 | tf_op jit(solution)/shard_map/kernel_pack/pallas_call | solution.py:281
  2.1 16.6 %all_to_all.20.atoms_ref = f32[16,8,128]{2,1,0:T(8,128)S(1)} all-to-all(f32[16,8,128]{2,1,0:T(8,128)} %get-tuple-element.8), channel_id=1, replica_groups=mesh['grp'=16,'pme'=64] {'grp'}, dimensions={0} | all-to-all | bytes 131072 | tf_op jit(solution)/shard_map/all_to_all | solution.py:328
  18.7 0.0 copy-done.2
  18.7 2.2 %kernel_spread.1 = bf16[64,8,128]{2,1,0:T(8,128)(2,1)S(1)} custom-call(f32[16,8,128]{2,1,0:T(8,128)S(1)} %all_to_all.20.atoms_ref, bf16[512,512]{1,0:T(8,128)(2,1)S(1)} %copy-done.2), custom_call_target="tpu_custom_call" | custom-call | flops 1073741824 | bytes 1048576 | tf_op jit(solution)/shard_map/kernel_spread/pallas_call | solution.py:305
  20.9 0.0 copy-start.1
  20.9 0.0 copy-start.3
  20.9 0.0 copy-start.4
  20.9 0.0 copy-start.5
  20.9 42.1 %all_to_all.21.mesh_ref = bf16[64,8,128]{2,1,0:T(8,128)(2,1)S(1)} all-to-all(bf16[64,8,128]{2,1,0:T(8,128)(2,1)S(1)} %kernel_spread.1), channel_id=1, replica_groups=mesh['grp'=16,'pme'=64] {'pme'}, dimensions={0} | all-to-all | bytes 262144 | tf_op jit(solution)/shard_map/all_to_all | solution.py:329
  63.1 0.0 copy-done.1
  63.1 0.0 copy-done.3
  63.1 0.0 copy-done.4
  63.1 0.0 copy-done.5
  63.1 0.8 kernel_waves.1
  63.9 22.3 %all_to_all.22.mesh_ref = bf16[64,8,128]{2,1,0:T(8,128)(2,1)S(1)} all-to-all(bf16[64,8,128]{2,1,0:T(8,128)(2,1)S(1)} %kernel_waves.1), channel_id=1, replica_groups=mesh['grp'=16,'pme'=64] {'pme'}, dimensions={0} | all-to-all | bytes 262144 | tf_op jit(solution)/shard_map/all_to_all | solution.py:330
  86.2 0.0 copy-start
  86.2 2.8 %kernel_sample.1 = f32[16,4,128]{2,1,0:T(4,128)S(1)} custom-call(f32[16,8,128]{2,1,0:T(8,128)S(1)} %all_to_all.20.atoms_ref, bf16[64,8,128]{2,1,0:T(8,128)(2,1)S(1)} %all_to_all.22.mesh_ref, bf16[512,512]{1,0:T(8,128)(2,1)S(1)} %copy-done.2), custom_call_target="tpu_custom_call" | custom-call | flops 1073741824 | bytes 1048576 | tf_op jit(solution)/shard_map/kernel_sample/pallas_call | solution.py:317
  89.0 10.2 %all_to_all.23.terms_ref = f32[16,4,128]{2,1,0:T(4,128)S(1)} all-to-all(f32[16,4,128]{2,1,0:T(4,128)S(1)} %kernel_sample.1), channel_id=1, replica_groups=mesh['grp'=16,'pme'=64] {'grp'}, dimensions={0} | all-to-all | bytes 65536 | tf_op jit(solution)/shard_map/all_to_all | solution.py:331
  99.2 0.0 copy-done
  99.2 0.6 kernel_total.1
Async XLA Ops:
  0.7 18.1 %copy-start.2 = (bf16[512,512]{1,0:T(8,128)(2,1)S(1)}, bf16[512,512]{1,0:T(8,128)(2,1)}, u32[]{:S(2)}) copy-start(bf16[512,512]{1,0:T(8,128)(2,1)} %constant.8.clone.table_ref) | copy-start | bytes 1572868
  20.9 42.2 %copy-start.1 = (f32[8,4,512]{2,1,0:T(4,128)S(1)}, f32[8,4,512]{2,1,0:T(4,128)}, u32[]{:S(2)}) copy-start(f32[8,4,512]{2,1,0:T(4,128)} %green_ref.1) | copy-start | bytes 196612
  20.9 42.2 %copy-start.3 = (bf16[128,256]{1,0:T(8,128)(2,1)S(1)}, bf16[128,256]{1,0:T(8,128)(2,1)}, u32[]{:S(2)}) copy-start(bf16[128,256]{1,0:T(8,128)(2,1)} %constant.9.clone.table_ref) | copy-start | bytes 196612
  20.9 42.1 %copy-start.4 = (f32[16,512]{1,0:T(8,128)S(1)}, f32[16,512]{1,0:T(8,128)}, u32[]{:S(2)}) copy-start(f32[16,512]{1,0:T(8,128)} %constant.11.clone.sin_ref) | copy-start | bytes 98308
  20.9 42.1 %copy-start.5 = (f32[16,512]{1,0:T(8,128)S(1)}, f32[16,512]{1,0:T(8,128)}, u32[]{:S(2)}) copy-start(f32[16,512]{1,0:T(8,128)} %constant.10.clone.cos_ref) | copy-start | bytes 98308
  86.2 13.0 %copy-start = (f32[4,128]{1,0:T(4,128)S(1)}, f32[4,128]{1,0:T(4,128)}, u32[]{:S(2)}) copy-start(f32[4,128]{1,0:T(4,128)} %get-tuple-element.7.factor_ref) | copy-start | bytes 6148
where the time goes:
time: 100 us; the launch traced here: 99.8 us
  blocking collectives  91.2 us (91%)
  Pallas kernels  7.79 us (8%)
    all_to_all x1, blocking collectives, body(): mesh = swap(spread(atoms), 'pme')  42.1 us
    all_to_all x1, blocking collectives, body(): mesh = swap(wave_product(mesh, green), 'pme')  22.3 us
    all_to_all x1, blocking collectives, body(): atoms = swap(packed, 'grp')  16.6 us
    all_to_all x1, blocking collectives, body(): terms = swap(sample(atoms, mesh), 'grp')  10.2 us
    pallas_call x1, Pallas kernels, sample(): return run(atoms, mesh, jnp.asarray(y_table()))  2.75 us
    pallas_call x1, Pallas kernels, spread(): return run(atoms, jnp.asarray(y_table()))  2.19 us

commit v1 on v0

--- a/solution.py
+++ b/solution.py
@@ -20,6 +20,8 @@
 PLANES = CZ + 3
 ATOMS = 128
 LANES = 128
+SPAN = 96
+SENT = (SLABS, 2, KY * SPAN)
 TWO_PI = 2.0 * math.pi
 
 f32 = jnp.float32
@@ -29,22 +31,21 @@
 
 @functools.cache
 def y_table():
-    wave = np.arange(NY).reshape(SLABS, 1, KY, 1)
-    angle = (wave * np.arange(NY).reshape(1, 1, 1, NY) % NY) * (TWO_PI / NY)
+    wave = np.arange(NY).reshape(SLABS, KY).T.reshape(KY, SLABS, 1)
+    angle = (wave * np.arange(NY) % NY) * (TWO_PI / NY)
     cosine, sine = np.cos(angle), np.sin(angle)
-    real = np.stack([cosine, sine], axis=3)
-    imag = np.stack([-sine, cosine], axis=3)
-    return np.concatenate([real, imag], axis=1).reshape(NY * 2, NY * 2).astype(jnp.bfloat16)
+    real = np.concatenate([cosine, sine], axis=2)
+    imag = np.concatenate([-sine, cosine], axis=2)
+    return np.stack([real, imag], axis=2).reshape(NY * 2, NY * 2).astype(jnp.bfloat16)
 
 
 @functools.cache
 def slab_table():
     angle = (np.arange(SLABS)[:, None] * np.arange(128)[None, :] % SLABS) * (TWO_PI / SLABS)
     cosine, sine = np.cos(angle), np.sin(angle)
-    table = np.concatenate(
-        [np.concatenate([cosine, -sine], axis=1), np.concatenate([sine, cosine], axis=1)], axis=0
-    )
-    return table.astype(jnp.bfloat16)
+    real = np.concatenate([cosine, -sine], axis=1)
+    imag = np.concatenate([sine, cosine], axis=1)
+    return np.stack([real, imag], axis=1).reshape(SLABS * 2, 256).astype(jnp.bfloat16)
 
 
 @functools.cache
@@ -171,20 +172,25 @@
     mesh = dot(y_ref[...], lead_ref[...], ((1,), (1,)))
     mesh = jnp.concatenate([mesh[:, :LANES], mesh[:, LANES:]], axis=0)
     waves = dot(table_ref[...], mesh.astype(bf16))
-    out_ref[...] = waves.reshape(SLABS, 2 * KY, LANES).astype(bf16)
-
-
-def kernel_waves(mesh_ref, green_ref, table_ref, cos_ref, sin_ref, out_ref, in_ref, hold_ref):
-    in_ref[...] = mesh_ref[...].astype(f32)
-    blank = jnp.zeros((LANES - PLANES * KX, 2 * LANES), f32)
+    rows = 2 * SLABS
+    lane = lax.broadcasted_iota(jnp.int32, (rows, LANES), 1)
+    turn = [waves[k * rows : (k + 1) * rows] for k in range(KY)]
+    turn = turn[:1] + [pltpu.roll(turn[k], LANES - k * (LANES - SPAN), 1) for k in range(1, KY)]
+    packed = [jnp.where(lane < LANES - (k + 1) * (LANES - SPAN), turn[k], turn[k + 1]) for k in range(KY - 1)]
+    out_ref[...] = jnp.concatenate(packed, axis=1).reshape(SENT).astype(bf16)
+
+
+def kernel_waves(mesh_ref, green_ref, table_ref, cos_ref, sin_ref, out_ref, part_ref, back_ref):
+    mesh = mesh_ref[...].reshape(2 * SLABS, KY * SPAN)
+    part_ref[...] = dot(mesh, table_ref[...], ((0,), (0,)))
+    blank = jnp.zeros((SPAN - PLANES * KX, 2 * LANES), f32)
     for k in range(KY):
-        slabs = jnp.concatenate([in_ref[:, k, :], in_ref[:, KY + k, :]], axis=0).astype(bf16)
-        part = dot(slabs, table_ref[...], ((0,), (0,)))
         real = [None] * 4
         imag = [None] * 4
         for z in range(PLANES):
-            a = part[z * KX : (z + 1) * KX, :LANES]
-            b = part[z * KX : (z + 1) * KX, LANES:]
+            at = k * SPAN + z * KX
+            a = part_ref[at : at + KX, :LANES]
+            b = part_ref[at : at + KX, LANES:]
             for m in range(4):
                 if z == 0:
                     real[m], imag[m] = a, b
@@ -209,11 +215,9 @@
                 a = a + (real[m] * c - imag[m] * s)
                 b = b + (imag[m] * c + real[m] * s)
             rows.append(jnp.concatenate([a, b], axis=1))
-        back = jnp.concatenate(rows + [blank], axis=0)
-        cells = dot(table_ref[...], back.astype(bf16), ((1,), (1,)))
-        hold_ref[:, k, :] = cells[:SLABS]
-        hold_ref[:, KY + k, :] = cells[SLABS:]
-    out_ref[...] = hold_ref[...].astype(bf16)
+        back_ref[k * SPAN : (k + 1) * SPAN] = jnp.concatenate(rows + [blank], axis=0).astype(bf16)
+    cells = dot(table_ref[...], back_ref[...], ((1,), (1,)))
+    out_ref[...] = cells.reshape(SENT).astype(bf16)
 
 
 def kernel_sample(atoms_ref, mesh_ref, table_ref, out_ref, y_ref):
@@ -224,7 +228,8 @@
     bx, by, bz = (whole(atoms_ref[:, 4 + d, :]) for d in range(3))
     y_at = lax.broadcasted_iota(jnp.int32, (NY, ATOMS), 0)
     z_at = lax.broadcasted_iota(jnp.int32, (16, ATOMS), 0)
-    waves = mesh_ref[...].reshape(2 * NY, LANES).T
+    waves = mesh_ref[...].reshape(2 * SLABS, KY * SPAN).T
+    waves = jnp.concatenate([waves[k * SPAN : (k + 1) * SPAN] for k in range(KY)], axis=1)
     cells = dot(waves, table_ref[...]).astype(bf16)
     used = PLANES * KX
     cells = jnp.concatenate([cells[:used, :NY], cells[:used, NY:]], axis=0)
@@ -301,13 +306,13 @@
 
 def spread(atoms):
     scratch = [pltpu.VMEM((NY, GROUPS * ATOMS), bf16), pltpu.VMEM((2 * LANES, GROUPS * ATOMS), bf16)]
-    run = call(kernel_spread, (SLABS, 2 * KY, LANES), bf16, 2, scratch, 1 << 30)
+    run = call(kernel_spread, SENT, bf16, 2, scratch, 1 << 30)
     return run(atoms, jnp.asarray(y_table()))
 
 
 def wave_product(mesh, green):
-    scratch = [pltpu.VMEM((SLABS, 2 * KY, LANES), f32)] * 2
-    run = call(kernel_waves, (SLABS, 2 * KY, LANES), bf16, 5, scratch, 1 << 30)
+    scratch = [pltpu.VMEM((KY * SPAN, 2 * LANES), f32), pltpu.VMEM((KY * SPAN, 2 * LANES), bf16)]
+    run = call(kernel_waves, SENT, bf16, 5, scratch, 1 << 30)
     return run(mesh, green, jnp.asarray(slab_table()), *map(jnp.asarray, plane_table()))
 
 

time: 100 us -> 97.7 us (0.977)
  blocking collectives: 91.2 us -> 88.6 us
    all_to_all x1, blocking collectives: 22.3 us -> 21 us  [body(): mesh = swap(wave_product(mesh, green), 'pme')]
    all_to_all x1, blocking collectives: 42.1 us -> 40.8 us  [body(): mesh = swap(spread(atoms), 'pme')]
where the time goes in v1:
time: 97.7 us; the launch traced here: 97.3 us
  blocking collectives  88.6 us (91%)
  Pallas kernels  7.94 us (8%)
    all_to_all x1, blocking collectives, body(): mesh = swap(spread(atoms), 'pme')  40.8 us
    all_to_all x1, blocking collectives, body(): mesh = swap(wave_product(mesh, green), 'pme')  21 us
    all_to_all x1, blocking collectives, body(): atoms = swap(packed, 'grp')  16.6 us
    all_to_all x1, blocking collectives, body(): terms = swap(sample(atoms, mesh), 'grp')  10.2 us
    pallas_call x1, Pallas kernels, sample(): return run(atoms, mesh, jnp.asarray(y_table()))  2.75 us
    pallas_call x1, Pallas kernels, spread(): return run(atoms, jnp.asarray(y_table()))  2.32 us

profile of v1, /device:TPU:1, one launch (start us, length us, event | category | flops | bytes accessed | tf_op | source)
XLA Modules:
  0.0 97.3 jit_solution(18306886630534935368)
XLA Ops:
  0.7 0.0 copy-start.2
  0.7 1.4 %kernel_pack.1 = (f32[16,8,128]{2,1,0:T(8,128)}, f32[4,128]{1,0:T(4,128)}) custom-call(s32[1]{0:T(128)S(6)} %copy.10.count_hbm, f32[1,128]{1,0:T(1,128)} %bitcast.1, f32[3,128]{1,0:T(4,128)} %frac_hbm.1, s32[3,128]{1,0:T(4,128)} %base_hbm.1), custom_call_target="tpu_custom_call" | custom-call | flops 1073741824 | bytes 1048576 | tf_op jit(solution)/shard_map/kernel_pack/pallas_call | solution.py:286
  2.1 16.6 %all_to_all.20.atoms_ref = f32[16,8,128]{2,1,0:T(8,128)S(1)} all-to-all(f32[16,8,128]{2,1,0:T(8,128)} %get-tuple-element.8), channel_id=1, replica_groups=mesh['grp'=16,'pme'=64] {'grp'}, dimensions={0} | all-to-all | bytes 131072 | tf_op jit(solution)/shard_map/all_to_all | solution.py:333
  18.7 0.0 copy-done.2
  18.7 2.3 %kernel_spread.1 = bf16[64,2,384]{2,1,0:T(2,128)(2,1)S(1)} custom-call(f32[16,8,128]{2,1,0:T(8,128)S(1)} %all_to_all.20.atoms_ref, bf16[512,512]{1,0:T(8,128)(2,1)S(1)} %copy-done.2), custom_call_target="tpu_custom_call" | custom-call | flops 1073741824 | bytes 1048576 | tf_op jit(solution)/shard_map/kernel_spread/pallas_call | solution.py:310
  21.0 0.0 copy-start.1
  21.0 0.0 copy-start.3
  21.1 0.0 copy-start.4
  21.1 0.0 copy-start.5
  21.1 40.8 %all_to_all.21.mesh_ref = bf16[64,2,384]{2,1,0:T(2,128)(2,1)S(1)} all-to-all(bf16[64,2,384]{2,1,0:T(2,128)(2,1)S(1)} %kernel_spread.1), channel_id=1, replica_groups=mesh['grp'=16,'pme'=64] {'pme'}, dimensions={0} | all-to-all | bytes 196608 | tf_op jit(solution)/shard_map/all_to_all | solution.py:334
  61.9 0.0 copy-done.1
  61.9 0.0 copy-done.3
  61.9 0.0 copy-done.4
  61.9 0.0 copy-done.5
  61.9 0.8 kernel_waves.1
  62.8 21.0 %all_to_all.22.mesh_ref = bf16[64,2,384]{2,1,0:T(2,128)(2,1)S(1)} all-to-all(bf16[64,2,384]{2,1,0:T(2,128)(2,1)S(1)} %kernel_waves.1), channel_id=1, replica_groups=mesh['grp'=16,'pme'=64] {'pme'}, dimensions={0} | all-to-all | bytes 196608 | tf_op jit(solution)/shard_map/all_to_all | solution.py:335
  83.8 0.0 copy-start
  83.8 2.8 %kernel_sample.1 = f32[16,4,128]{2,1,0:T(4,128)S(1)} custom-call(f32[16,8,128]{2,1,0:T(8,128)S(1)} %all_to_all.20.atoms_ref, bf16[64,2,384]{2,1,0:T(2,128)(2,1)S(1)} %all_to_all.22.mesh_ref, bf16[512,512]{1,0:T(8,128)(2,1)S(1)} %copy-done.2), custom_call_target="tpu_custom_call" | custom-call | flops 1073741824 | bytes 1048576 | tf_op jit(solution)/shard_map/kernel_sample/pallas_call | solution.py:322
  86.6 10.2 %all_to_all.23.terms_ref = f32[16,4,128]{2,1,0:T(4,128)S(1)} all-to-all(f32[16,4,128]{2,1,0:T(4,128)S(1)} %kernel_sample.1), channel_id=1, replica_groups=mesh['grp'=16,'pme'=64] {'grp'}, dimensions={0} | all-to-all | bytes 65536 | tf_op jit(solution)/shard_map/all_to_all | solution.py:336
  96.7 0.0 copy-done
  96.7 0.6 kernel_total.1
Async XLA Ops:
  0.7 18.1 %copy-start.2 = (bf16[512,512]{1,0:T(8,128)(2,1)S(1)}, bf16[512,512]{1,0:T(8,128)(2,1)}, u32[]{:S(2)}) copy-start(bf16[512,512]{1,0:T(8,128)(2,1)} %constant.8.clone.table_ref) | copy-start | bytes 1572868
  21.0 40.9 %copy-start.1 = (f32[8,4,512]{2,1,0:T(4,128)S(1)}, f32[8,4,512]{2,1,0:T(4,128)}, u32[]{:S(2)}) copy-start(f32[8,4,512]{2,1,0:T(4,128)} %green_ref.1) | copy-start | bytes 196612
  21.0 40.9 %copy-start.3 = (bf16[128,256]{1,0:T(8,128)(2,1)S(1)}, bf16[128,256]{1,0:T(8,128)(2,1)}, u32[]{:S(2)}) copy-start(bf16[128,256]{1,0:T(8,128)(2,1)} %constant.9.clone.table_ref) | copy-start | bytes 196612
  21.1 40.9 %copy-start.4 = (f32[16,512]{1,0:T(8,128)S(1)}, f32[16,512]{1,0:T(8,128)}, u32[]{:S(2)}) copy-start(f32[16,512]{1,0:T(8,128)} %constant.11.clone.sin_ref) | copy-start | bytes 98308
  21.1 40.8 %copy-start.5 = (f32[16,512]{1,0:T(8,128)S(1)}, f32[16,512]{1,0:T(8,128)}, u32[]{:S(2)}) copy-start(f32[16,512]{1,0:T(8,128)} %constant.10.clone.cos_ref) | copy-start | bytes 98308
  83.8 13.0 %copy-start = (f32[4,128]{1,0:T(4,128)S(1)}, f32[4,128]{1,0:T(4,128)}, u32[]{:S(2)}) copy-start(f32[4,128]{1,0:T(4,128)} %get-tuple-element.7.factor_ref) | copy-start | bytes 6148

commit v2 on v1

--- a/solution.py
+++ b/solution.py
@@ -126,8 +126,25 @@
     return out
 
 
-def kernel_pack(count_hbm, charge_hbm, frac_hbm, base_hbm, out_ref, factor_ref, count_ref, charge_ref, frac_ref, base_ref, sems):
-    moves = ((count_hbm, count_ref), (charge_hbm, charge_ref), (frac_hbm, frac_ref), (base_hbm, base_ref))
+def y_rows(at, cells, weights, g):
+    out = jnp.zeros(at.shape, bf16)
+    for j in range(4):
+        cell = jnp.broadcast_to(row(cells[j], g), (16, ATOMS)).astype(bf16)
+        weight = jnp.broadcast_to(row(weights[j], g), (16, ATOMS)).astype(bf16)
+        out = jnp.where(at == tall(cell), tall(weight), out)
+    return out
+
+
+def tall(block):
+    return jnp.concatenate([block] * (NY // 16), axis=0)
+
+
+def y_cells(by):
+    return [((by + j) & (NY - 1)).astype(f32) for j in range(4)]
+
+
+def kernel_pack(count_ref, charge_hbm, frac_hbm, base_hbm, out_ref, factor_ref, charge_ref, frac_ref, base_ref, sems):
+    moves = ((charge_hbm, charge_ref), (frac_hbm, frac_ref), (base_hbm, base_ref))
     copies = [pltpu.make_async_copy(a, b, sems.at[i]) for i, (a, b) in enumerate(moves)]
     for copy in copies:
         copy.start()
@@ -155,13 +172,14 @@
     charge = atoms_ref[:, 0, :]
     wx, wy, wz = (spline(atoms_ref[:, 1 + d, :]) for d in range(3))
     bx, by, bz = (whole(atoms_ref[:, 4 + d, :]) for d in range(3))
-    y_at = lax.broadcasted_iota(jnp.int32, (NY, ATOMS), 0)
+    y_at = lax.broadcasted_iota(jnp.int32, (NY, ATOMS), 0).astype(f32).astype(bf16)
+    ys = y_cells(by)
     z_at = lax.broadcasted_iota(jnp.int32, (16, ATOMS), 0)
     wz = [charge * w for w in wz]
     blank = jnp.zeros((LANES - PLANES * KX, ATOMS), f32)
     for g in range(GROUPS):
         here = pl.ds(g * ATOMS, ATOMS)
-        y_ref[:, here] = placed((y_at - row(by, g)) & (NY - 1), wy, g).astype(bf16)
+        y_ref[:, here] = y_rows(y_at, ys, wy, g)
         start = unit_circle((kx * row(bx, g)) & (NX - 1))
         real, imag = turned(start, x_terms(wx, g, steps))
         z = placed(z_at - row(bz, g), wz, g)
@@ -177,7 +195,7 @@
     turn = [waves[k * rows : (k + 1) * rows] for k in range(KY)]
     turn = turn[:1] + [pltpu.roll(turn[k], LANES - k * (LANES - SPAN), 1) for k in range(1, KY)]
     packed = [jnp.where(lane < LANES - (k + 1) * (LANES - SPAN), turn[k], turn[k + 1]) for k in range(KY - 1)]
-    out_ref[...] = jnp.concatenate(packed, axis=1).reshape(SENT).astype(bf16)
+    out_ref[...] = jnp.concatenate(packed, axis=1).astype(bf16).reshape(SENT)
 
 
 def kernel_waves(mesh_ref, green_ref, table_ref, cos_ref, sin_ref, out_ref, part_ref, back_ref):
@@ -217,7 +235,7 @@
             rows.append(jnp.concatenate([a, b], axis=1))
         back_ref[k * SPAN : (k + 1) * SPAN] = jnp.concatenate(rows + [blank], axis=0).astype(bf16)
     cells = dot(table_ref[...], back_ref[...], ((1,), (1,)))
-    out_ref[...] = cells.reshape(SENT).astype(bf16)
+    out_ref[...] = cells.astype(bf16).reshape(SENT)
 
 
 def kernel_sample(atoms_ref, mesh_ref, table_ref, out_ref, y_ref):
@@ -226,7 +244,8 @@
     wx, wy, wz = (spline(atoms_ref[:, 1 + d, :]) for d in range(3))
     dx, dy, dz = (spline_slopes(atoms_ref[:, 1 + d, :]) for d in range(3))
     bx, by, bz = (whole(atoms_ref[:, 4 + d, :]) for d in range(3))
-    y_at = lax.broadcasted_iota(jnp.int32, (NY, ATOMS), 0)
+    y_at = lax.broadcasted_iota(jnp.int32, (NY, ATOMS), 0).astype(f32).astype(bf16)
+    ys = y_cells(by)
     z_at = lax.broadcasted_iota(jnp.int32, (16, ATOMS), 0)
     waves = mesh_ref[...].reshape(2 * SLABS, KY * SPAN).T
     waves = jnp.concatenate([waves[k * SPAN : (k + 1) * SPAN] for k in range(KY)], axis=1)
@@ -234,9 +253,8 @@
     used = PLANES * KX
     cells = jnp.concatenate([cells[:used, :NY], cells[:used, NY:]], axis=0)
     for g in range(GROUPS):
-        rel = (y_at - row(by, g)) & (NY - 1)
-        y_ref[:, 0:ATOMS] = placed(rel, wy, g).astype(bf16)
-        y_ref[:, ATOMS : 2 * ATOMS] = placed(rel, dy, g).astype(bf16)
+        y_ref[:, 0:ATOMS] = y_rows(y_at, ys, wy, g)
+        y_ref[:, ATOMS : 2 * ATOMS] = y_rows(y_at, ys, dy, g)
         values = dot(cells, y_ref[...])
         start = unit_circle((kx * row(bx, g)) & (NX - 1))
         x_real, x_imag = turned(start, x_terms(wx, g, steps))
@@ -289,19 +307,18 @@
             jax.ShapeDtypeStruct((GROUPS, 8, ATOMS), f32),
             jax.ShapeDtypeStruct((4, ATOMS), f32),
         ],
-        in_specs=[pl.BlockSpec(memory_space=pltpu.HBM)] * 4,
+        in_specs=[pl.BlockSpec(memory_space=pltpu.SMEM)] + [pl.BlockSpec(memory_space=pltpu.HBM)] * 3,
         out_specs=[VMEM, VMEM],
         scratch_shapes=[
-            pltpu.SMEM((1,), jnp.int32),
             pltpu.VMEM((1, ATOMS), f32),
             pltpu.VMEM((3, ATOMS), f32),
             pltpu.VMEM((3, ATOMS), jnp.int32),
-            pltpu.SemaphoreType.DMA((4,)),
+            pltpu.SemaphoreType.DMA((3,)),
         ],
         name="kernel_pack",
-        compiler_params=pltpu.CompilerParams(vmem_limit_bytes=60 << 20),
+        compiler_params=pltpu.CompilerParams(vmem_limit_bytes=4 << 20),
         cost_estimate=pl.CostEstimate(flops=1 << 30, bytes_accessed=1 << 20, transcendentals=0),
-    )(counts, charge, frac, base)
+    )(counts, *(pltpu.with_memory_space_constraint(a, pltpu.HBM) for a in (charge, frac, base)))
 
 
 def spread(atoms):

time: 97.7 us -> 95.6 us (0.979)
  Pallas kernels: 7.94 us -> 6.08 us
where the time goes in v2:
time: 95.6 us; the launch traced here: 95.3 us
  blocking collectives  88.4 us (92%)
  Pallas kernels  6.08 us (6%)
    all_to_all x1, blocking collectives, body(): mesh = swap(spread(atoms), 'pme')  40.8 us
    all_to_all x1, blocking collectives, body(): mesh = swap(wave_product(mesh, green), 'pme')  21 us
    all_to_all x1, blocking collectives, body(): atoms = swap(packed, 'grp')  16.4 us
    all_to_all x1, blocking collectives, body(): terms = swap(sample(atoms, mesh), 'grp')  10.2 us
    pallas_call x1, Pallas kernels, sample(): return run(atoms, mesh, jnp.asarray(y_table()))  2.09 us

profile of v2, /device:TPU:1, one launch (start us, length us, event | category | flops | bytes accessed | tf_op | source)
XLA Modules:
  0.0 95.3 jit_solution(11084042538148682766)
XLA Ops:
  0.7 0.0 copy-start.1
  0.7 0.8 kernel_pack.1
  1.5 16.4 %all_to_all.20.atoms_ref = f32[16,8,128]{2,1,0:T(8,128)S(1)} all-to-all(f32[16,8,128]{2,1,0:T(8,128)S(1)} %get-tuple-element.8), channel_id=1, replica_groups=mesh['grp'=16,'pme'=64] {'grp'}, dimensions={0} | all-to-all | bytes 131072 | tf_op jit(solution)/shard_map/all_to_all | solution.py:350
  17.8 0.0 copy-done.1
  17.9 1.8 %kernel_spread.1 = bf16[64,2,384]{2,1,0:T(2,128)(2,1)S(1)} custom-call(f32[16,8,128]{2,1,0:T(8,128)S(1)} %all_to_all.20.atoms_ref, bf16[512,512]{1,0:T(8,128)(2,1)S(1)} %copy-done.1), custom_call_target="tpu_custom_call" | custom-call | flops 1073741824 | bytes 1048576 | tf_op jit(solution)/shard_map/kernel_spread/pallas_call | solution.py:327
  19.7 0.0 copy-start
  19.7 0.0 copy-start.2
  19.7 0.0 copy-start.3
  19.7 0.0 copy-start.4
  19.7 40.8 %all_to_all.21.mesh_ref = bf16[64,2,384]{2,1,0:T(2,128)(2,1)S(1)} all-to-all(bf16[64,2,384]{2,1,0:T(2,128)(2,1)S(1)} %kernel_spread.1), channel_id=1, replica_groups=mesh['grp'=16,'pme'=64] {'pme'}, dimensions={0} | all-to-all | bytes 196608 | tf_op jit(solution)/shard_map/all_to_all | solution.py:351
  60.6 0.0 copy-done
  60.6 0.0 copy-done.2
  60.6 0.0 copy-done.3
  60.6 0.0 copy-done.4
  60.6 0.7 kernel_waves.1
  61.3 21.0 %all_to_all.22.mesh_ref = bf16[64,2,384]{2,1,0:T(2,128)(2,1)S(1)} all-to-all(bf16[64,2,384]{2,1,0:T(2,128)(2,1)S(1)} %kernel_waves.1), channel_id=1, replica_groups=mesh['grp'=16,'pme'=64] {'pme'}, dimensions={0} | all-to-all | bytes 196608 | tf_op jit(solution)/shard_map/all_to_all | solution.py:352
  82.4 2.1 %kernel_sample.1 = f32[16,4,128]{2,1,0:T(4,128)S(1)} custom-call(f32[16,8,128]{2,1,0:T(8,128)S(1)} %all_to_all.20.atoms_ref, bf16[64,2,384]{2,1,0:T(2,128)(2,1)S(1)} %all_to_all.22.mesh_ref, bf16[512,512]{1,0:T(8,128)(2,1)S(1)} %copy-done.1), custom_call_target="tpu_custom_call" | custom-call | flops 1073741824 | bytes 1048576 | tf_op jit(solution)/shard_map/kernel_sample/pallas_call | solution.py:339
  84.5 10.2 %all_to_all.23.terms_ref = f32[16,4,128]{2,1,0:T(4,128)S(1)} all-to-all(f32[16,4,128]{2,1,0:T(4,128)S(1)} %kernel_sample.1), channel_id=1, replica_groups=mesh['grp'=16,'pme'=64] {'grp'}, dimensions={0} | all-to-all | bytes 65536 | tf_op jit(solution)/shard_map/all_to_all | solution.py:353
  94.7 0.6 kernel_total.1
Async XLA Ops:
  0.7 17.2 %copy-start.1 = (bf16[512,512]{1,0:T(8,128)(2,1)S(1)}, bf16[512,512]{1,0:T(8,128)(2,1)}, u32[]{:S(2)}) copy-start(bf16[512,512]{1,0:T(8,128)(2,1)} %constant.8.clone.table_ref) | copy-start | bytes 1572868
  19.7 40.9 %copy-start = (f32[8,4,512]{2,1,0:T(4,128)S(1)}, f32[8,4,512]{2,1,0:T(4,128)}, u32[]{:S(2)}) copy-start(f32[8,4,512]{2,1,0:T(4,128)} %green_ref.1) | copy-start | bytes 196612
  19.7 40.9 %copy-start.2 = (bf16[128,256]{1,0:T(8,128)(2,1)S(1)}, bf16[128,256]{1,0:T(8,128)(2,1)}, u32[]{:S(2)}) copy-start(bf16[128,256]{1,0:T(8,128)(2,1)} %constant.9.clone.table_ref) | copy-start | bytes 196612
  19.7 40.9 %copy-start.3 = (f32[16,512]{1,0:T(8,128)S(1)}, f32[16,512]{1,0:T(8,128)}, u32[]{:S(2)}) copy-start(f32[16,512]{1,0:T(8,128)} %constant.11.clone.sin_ref) | copy-start | bytes 98308
  19.7 40.8 %copy-start.4 = (f32[16,512]{1,0:T(8,128)S(1)}, f32[16,512]{1,0:T(8,128)}, u32[]{:S(2)}) copy-start(f32[16,512]{1,0:T(8,128)} %constant.10.clone.cos_ref) | copy-start | bytes 98308

commit v3 on v2

--- a/solution.py
+++ b/solution.py
@@ -166,7 +166,7 @@
     return whole(atoms_ref[0, 7:8, :]) * KX + lax.broadcasted_iota(jnp.int32, (KX, ATOMS), 0)
 
 
-def kernel_spread(atoms_ref, table_ref, out_ref, y_ref, lead_ref):
+def kernel_spread(atoms_ref, table_ref, out_ref, y_ref, x_ref, lead_ref):
     kx = own_waves(atoms_ref)
     steps = x_steps(kx)
     charge = atoms_ref[:, 0, :]
@@ -182,6 +182,8 @@
         y_ref[:, here] = y_rows(y_at, ys, wy, g)
         start = unit_circle((kx * row(bx, g)) & (NX - 1))
         real, imag = turned(start, x_terms(wx, g, steps))
+        for k, values in enumerate((real, imag) + start):
+            x_ref[k, :, here] = values
         z = placed(z_at - row(bz, g), wz, g)
         lead = [row(z, k) * real for k in range(PLANES)] + [blank]
         lead_ref[0:LANES, here] = jnp.concatenate(lead, axis=0).astype(bf16)
@@ -238,12 +240,12 @@
     out_ref[...] = cells.astype(bf16).reshape(SENT)
 
 
-def kernel_sample(atoms_ref, mesh_ref, table_ref, out_ref, y_ref):
+def kernel_sample(atoms_ref, mesh_ref, table_ref, y_ref, x_ref, out_ref, slope_ref):
     kx = own_waves(atoms_ref)
     steps = x_steps(kx)
-    wx, wy, wz = (spline(atoms_ref[:, 1 + d, :]) for d in range(3))
+    wz = spline(atoms_ref[:, 3, :])
     dx, dy, dz = (spline_slopes(atoms_ref[:, 1 + d, :]) for d in range(3))
-    bx, by, bz = (whole(atoms_ref[:, 4 + d, :]) for d in range(3))
+    by, bz = (whole(atoms_ref[:, 4 + d, :]) for d in range(1, 3))
     y_at = lax.broadcasted_iota(jnp.int32, (NY, ATOMS), 0).astype(f32).astype(bf16)
     ys = y_cells(by)
     z_at = lax.broadcasted_iota(jnp.int32, (16, ATOMS), 0)
@@ -252,12 +254,9 @@
     cells = dot(waves, table_ref[...]).astype(bf16)
     used = PLANES * KX
     cells = jnp.concatenate([cells[:used, :NY], cells[:used, NY:]], axis=0)
-    for g in range(GROUPS):
-        y_ref[:, 0:ATOMS] = y_rows(y_at, ys, wy, g)
-        y_ref[:, ATOMS : 2 * ATOMS] = y_rows(y_at, ys, dy, g)
-        values = dot(cells, y_ref[...])
-        start = unit_circle((kx * row(bx, g)) & (NX - 1))
-        x_real, x_imag = turned(start, x_terms(wx, g, steps))
+
+    def sample_block(g, level, slope):
+        x_real, x_imag, *start = (x_ref[k, :, pl.ds(g * ATOMS, ATOMS)] for k in range(4))
         s_real, s_imag = turned(start, x_terms(dx, g, steps))
         z = placed(z_at - row(bz, g), wz, g)
         dzt = placed(z_at - row(bz, g), dz, g)
@@ -267,10 +266,11 @@
         for part in range(2):
             for k in range(PLANES):
                 at = part * used + k * KX
-                here = values[at : at + KX]
-                plain[part] = plain[part] + row(z, k) * here[:, :ATOMS]
-                along_y[part] = along_y[part] + row(z, k) * here[:, ATOMS:]
-                along_z[part] = along_z[part] + row(dzt, k) * here[:, :ATOMS]
+                here = level[at : at + KX]
+                there = slope[at : at + KX]
+                plain[part] = plain[part] + row(z, k) * here
+                along_y[part] = along_y[part] + row(z, k) * there
+                along_z[part] = along_z[part] + row(dzt, k) * here
         terms = (
             x_real * plain[0] + x_imag * plain[1],
             s_real * plain[0] + s_imag * plain[1],
@@ -278,6 +278,18 @@
             x_real * along_z[0] + x_imag * along_z[1],
         )
         out_ref[g] = jnp.concatenate([jnp.sum(t, axis=0, keepdims=True) for t in terms], axis=0)
+
+    for g in range(GROUPS):
+        here = pl.ds(g * ATOMS, ATOMS)
+        slope_ref[:, here] = y_rows(y_at, ys, dy, g)
+        if g % 2 == 0:
+            continue
+        both = pl.ds((g - 1) * ATOMS, 2 * ATOMS)
+        level = dot(cells, y_ref[:, both])
+        slope = dot(cells, slope_ref[:, both])
+        for h in range(2):
+            at = slice(h * ATOMS, (h + 1) * ATOMS)
+            sample_block(g - 1 + h, level[:, at], slope[:, at])
 
 
 def kernel_total(factor_ref, terms_ref, out_ref):
@@ -322,9 +334,20 @@
 
 
 def spread(atoms):
-    scratch = [pltpu.VMEM((NY, GROUPS * ATOMS), bf16), pltpu.VMEM((2 * LANES, GROUPS * ATOMS), bf16)]
-    run = call(kernel_spread, SENT, bf16, 2, scratch, 1 << 30)
-    return run(atoms, jnp.asarray(y_table()))
+    return pl.pallas_call(
+        kernel_spread,
+        out_shape=[
+            jax.ShapeDtypeStruct(SENT, bf16),
+            jax.ShapeDtypeStruct((NY, GROUPS * ATOMS), bf16),
+            jax.ShapeDtypeStruct((4, KX, GROUPS * ATOMS), f32),
+        ],
+        in_specs=[VMEM] * 2,
+        out_specs=[VMEM] * 3,
+        scratch_shapes=[pltpu.VMEM((2 * LANES, GROUPS * ATOMS), bf16)],
+        name="kernel_spread",
+        compiler_params=pltpu.CompilerParams(vmem_limit_bytes=8 << 20),
+        cost_estimate=pl.CostEstimate(flops=1 << 30, bytes_accessed=1 << 20, transcendentals=0),
+    )(atoms, jnp.asarray(y_table()))
 
 
 def wave_product(mesh, green):
@@ -333,10 +356,10 @@
     return run(mesh, green, jnp.asarray(slab_table()), *map(jnp.asarray, plane_table()))
 
 
-def sample(atoms, mesh):
-    scratch = [pltpu.VMEM((NY, 2 * ATOMS), bf16)]
-    run = call(kernel_sample, (GROUPS, 4, ATOMS), f32, 3, scratch, 1 << 30)
-    return run(atoms, mesh, jnp.asarray(y_table()))
+def sample(atoms, mesh, y_weights, x_sums):
+    scratch = [pltpu.VMEM((NY, GROUPS * ATOMS), bf16)]
+    run = call(kernel_sample, (GROUPS, 4, ATOMS), f32, 5, scratch, 1 << 30)
+    return run(atoms, mesh, jnp.asarray(y_table()), y_weights, x_sums)
 
 
 def total(factors, terms):
@@ -348,9 +371,10 @@
     swap = functools.partial(lax.all_to_all, split_axis=0, concat_axis=0, tiled=True)
     packed, factors = pack(counts, charge, frac, base)
     atoms = swap(packed, "grp")
-    mesh = swap(spread(atoms), "pme")
+    mesh, y_weights, x_sums = spread(atoms)
+    mesh = swap(mesh, "pme")
     mesh = swap(wave_product(mesh, green), "pme")
-    terms = swap(sample(atoms, mesh), "grp")
+    terms = swap(sample(atoms, mesh, y_weights, x_sums), "grp")
     return total(factors, terms)
 
 

time: 95.6 us -> 95.1 us (level)
  no operation moved by 1% of the time
where the time goes in v3:
time: 95.1 us; the launch traced here: 94.8 us
  blocking collectives  88.4 us (93%)
  Pallas kernels  5.58 us (6%)
    all_to_all x1, blocking collectives, body(): mesh = swap(mesh, 'pme')  40.8 us
    all_to_all x1, blocking collectives, body(): mesh = swap(wave_product(mesh, green), 'pme')  21 us
    all_to_all x1, blocking collectives, body(): atoms = swap(packed, 'grp')  16.4 us
    all_to_all x1, blocking collectives, body(): terms = swap(sample(atoms, mesh, y_weights, x_sums), 'grp')  10.2 us

profile of v3, /device:TPU:1, one launch (start us, length us, event | category | flops | bytes accessed | tf_op | source)
XLA Modules:
  0.0 94.8 jit_solution(1948381606673172291)
XLA Ops:
  0.7 0.0 copy-start.1
  0.7 0.8 kernel_pack.1
  1.5 16.4 %all_to_all.20.atoms_ref = f32[16,8,128]{2,1,0:T(8,128)S(1)} all-to-all(f32[16,8,128]{2,1,0:T(8,128)S(1)} %get-tuple-element.11), channel_id=1, replica_groups=mesh['grp'=16,'pme'=64] {'grp'}, dimensions={0} | all-to-all | bytes 131072 | tf_op jit(solution)/shard_map/all_to_all | solution.py:373
  17.8 0.0 copy-done.1
  17.9 1.9 %kernel_spread.1 = (bf16[64,2,384]{2,1,0:T(2,128)(2,1)S(1)}, bf16[256,2048]{1,0:T(8,128)(2,1)S(1)}, f32[4,8,2048]{2,1,0:T(8,128)S(1)}) custom-call(f32[16,8,128]{2,1,0:T(8,128)S(1)} %all_to_all.20.atoms_ref, bf16[512,512]{1,0:T(8,128)(2,1)S(1)} %copy-done.1), custom_call_target="tpu_custom_call" | custom-call | flops 1073741824 | bytes 1048576 | tf_op jit(solution)/shard_map/kernel_spread/pallas_call | solution.py:337
  19.7 0.0 copy-start
  19.7 0.0 copy-start.2
  19.8 0.0 copy-start.3
  19.8 0.0 copy-start.4
  19.8 40.8 %all_to_all.21.mesh_ref = bf16[64,2,384]{2,1,0:T(2,128)(2,1)S(1)} all-to-all(bf16[64,2,384]{2,1,0:T(2,128)(2,1)S(1)} %get-tuple-element.12), channel_id=1, replica_groups=mesh['grp'=16,'pme'=64] {'pme'}, dimensions={0} | all-to-all | bytes 196608 | tf_op jit(solution)/shard_map/all_to_all | solution.py:375
  60.6 0.0 copy-done
  60.6 0.0 copy-done.2
  60.6 0.0 copy-done.3
  60.6 0.0 copy-done.4
  60.6 0.7 kernel_waves.1
  61.4 21.0 %all_to_all.22.mesh_ref = bf16[64,2,384]{2,1,0:T(2,128)(2,1)S(1)} all-to-all(bf16[64,2,384]{2,1,0:T(2,128)(2,1)S(1)} %kernel_waves.1), channel_id=1, replica_groups=mesh['grp'=16,'pme'=64] {'pme'}, dimensions={0} | all-to-all | bytes 196608 | tf_op jit(solution)/shard_map/all_to_all | solution.py:376
  82.4 1.6 %kernel_sample.1 = f32[16,4,128]{2,1,0:T(4,128)S(1)} custom-call(f32[16,8,128]{2,1,0:T(8,128)S(1)} %all_to_all.20.atoms_ref, bf16[64,2,384]{2,1,0:T(2,128)(2,1)S(1)} %all_to_all.22.mesh_ref, bf16[512,512]{1,0:T(8,128)(2,1)S(1)} %copy-done.1, bf16[256,2048]{1,0:T(8,128)(2,1)S(1)} %get-tuple-element.13.y_ref, f32[4,8,2048]{2,1,0:T(8,128)S(1)} %get-tuple-element.14.x_ref), custom_call_target="tpu_custom_call" | custom-call | flops 1073741824 | bytes 1048576 | tf_op jit(solution)/shard_map/kernel_sample/pallas_call | solution.py:362
  84.0 10.2 %all_to_all.23.terms_ref = f32[16,4,128]{2,1,0:T(4,128)S(1)} all-to-all(f32[16,4,128]{2,1,0:T(4,128)S(1)} %kernel_sample.1), channel_id=1, replica_groups=mesh['grp'=16,'pme'=64] {'grp'}, dimensions={0} | all-to-all | bytes 65536 | tf_op jit(solution)/shard_map/all_to_all | solution.py:377
  94.2 0.6 kernel_total.1
Async XLA Ops:
  0.7 17.2 %copy-start.1 = (bf16[512,512]{1,0:T(8,128)(2,1)S(1)}, bf16[512,512]{1,0:T(8,128)(2,1)}, u32[]{:S(2)}) copy-start(bf16[512,512]{1,0:T(8,128)(2,1)} %constant.8.clone.table_ref) | copy-start | bytes 1572868
  19.7 40.9 %copy-start = (f32[8,4,512]{2,1,0:T(4,128)S(1)}, f32[8,4,512]{2,1,0:T(4,128)}, u32[]{:S(2)}) copy-start(f32[8,4,512]{2,1,0:T(4,128)} %green_ref.1) | copy-start | bytes 196612
  19.7 40.9 %copy-start.2 = (bf16[128,256]{1,0:T(8,128)(2,1)S(1)}, bf16[128,256]{1,0:T(8,128)(2,1)}, u32[]{:S(2)}) copy-start(bf16[128,256]{1,0:T(8,128)(2,1)} %constant.9.clone.table_ref) | copy-start | bytes 196612
  19.8 40.9 %copy-start.3 = (f32[16,512]{1,0:T(8,128)S(1)}, f32[16,512]{1,0:T(8,128)}, u32[]{:S(2)}) copy-start(f32[16,512]{1,0:T(8,128)} %constant.11.clone.sin_ref) | copy-start | bytes 98308
  19.8 40.8 %copy-start.4 = (f32[16,512]{1,0:T(8,128)S(1)}, f32[16,512]{1,0:T(8,128)}, u32[]{:S(2)}) copy-start(f32[16,512]{1,0:T(8,128)} %constant.10.clone.cos_ref) | copy-start | bytes 98308

commit v4 on v3

--- a/solution.py
+++ b/solution.py
@@ -126,21 +126,24 @@
     return out
 
 
-def y_rows(at, cells, weights, g):
-    out = jnp.zeros(at.shape, bf16)
+def y_rows(spots, weights, g):
+    block, local, *weights = (
+        jnp.broadcast_to(row(v, g), (16, ATOMS)).astype(bf16) for v in (*spots, *weights)
+    )
+    nothing = jnp.zeros((16, ATOMS), bf16)
+    rel = lax.broadcasted_iota(jnp.int32, (16, ATOMS), 0).astype(f32).astype(bf16) - local
+    low = high = nothing
     for j in range(4):
-        cell = jnp.broadcast_to(row(cells[j], g), (16, ATOMS)).astype(bf16)
-        weight = jnp.broadcast_to(row(weights[j], g), (16, ATOMS)).astype(bf16)
-        out = jnp.where(at == tall(cell), tall(weight), out)
-    return out
-
-
-def tall(block):
-    return jnp.concatenate([block] * (NY // 16), axis=0)
-
-
-def y_cells(by):
-    return [((by + j) & (NY - 1)).astype(f32) for j in range(4)]
+        low = jnp.where(rel == j, weights[j], low)
+        high = jnp.where(rel == j - 16, weights[j], high)
+    own = [block == b for b in range(16)]
+    return jnp.concatenate(
+        [jnp.where(own[b], low, jnp.where(own[b - 1], high, nothing)) for b in range(16)], axis=0
+    )
+
+
+def y_spots(by):
+    return (by >> 4).astype(f32), (by & 15).astype(f32)
 
 
 def kernel_pack(count_ref, charge_hbm, frac_hbm, base_hbm, out_ref, factor_ref, charge_ref, frac_ref, base_ref, sems):
@@ -172,14 +175,13 @@
     charge = atoms_ref[:, 0, :]
     wx, wy, wz = (spline(atoms_ref[:, 1 + d, :]) for d in range(3))
     bx, by, bz = (whole(atoms_ref[:, 4 + d, :]) for d in range(3))
-    y_at = lax.broadcasted_iota(jnp.int32, (NY, ATOMS), 0).astype(f32).astype(bf16)
-    ys = y_cells(by)
+    ys = y_spots(by)
     z_at = lax.broadcasted_iota(jnp.int32, (16, ATOMS), 0)
     wz = [charge * w for w in wz]
     blank = jnp.zeros((LANES - PLANES * KX, ATOMS), f32)
     for g in range(GROUPS):
         here = pl.ds(g * ATOMS, ATOMS)
-        y_ref[:, here] = y_rows(y_at, ys, wy, g)
+        y_ref[:, here] = y_rows(ys, wy, g)
         start = unit_circle((kx * row(bx, g)) & (NX - 1))
         real, imag = turned(start, x_terms(wx, g, steps))
         for k, values in enumerate((real, imag) + start):
@@ -246,8 +248,7 @@
     wz = spline(atoms_ref[:, 3, :])
     dx, dy, dz = (spline_slopes(atoms_ref[:, 1 + d, :]) for d in range(3))
     by, bz = (whole(atoms_ref[:, 4 + d, :]) for d in range(1, 3))
-    y_at = lax.broadcasted_iota(jnp.int32, (NY, ATOMS), 0).astype(f32).astype(bf16)
-    ys = y_cells(by)
+    ys = y_spots(by)
     z_at = lax.broadcasted_iota(jnp.int32, (16, ATOMS), 0)
     waves = mesh_ref[...].reshape(2 * SLABS, KY * SPAN).T
     waves = jnp.concatenate([waves[k * SPAN : (k + 1) * SPAN] for k in range(KY)], axis=1)
@@ -281,7 +282,7 @@
 
     for g in range(GROUPS):
         here = pl.ds(g * ATOMS, ATOMS)
-        slope_ref[:, here] = y_rows(y_at, ys, dy, g)
+        slope_ref[:, here] = y_rows(ys, dy, g)
         if g % 2 == 0:
             continue
         both = pl.ds((g - 1) * ATOMS, 2 * ATOMS)

time: 95.1 us -> 94.7 us (level)
  no operation moved by 1% of the time
where the time goes in v4:
time: 94.7 us; the launch traced here: 94.4 us
  blocking collectives  88.4 us (93%)
  Pallas kernels  5.2 us (5%)
    all_to_all x1, blocking collectives, body(): mesh = swap(mesh, 'pme')  40.8 us
    all_to_all x1, blocking collectives, body(): mesh = swap(wave_product(mesh, green), 'pme')  21 us
    all_to_all x1, blocking collectives, body(): atoms = swap(packed, 'grp')  16.4 us
    all_to_all x1, blocking collectives, body(): terms = swap(sample(atoms, mesh, y_weights, x_sums), 'grp')  10.2 us

profile of v4, /device:TPU:1, one launch (start us, length us, event | category | flops | bytes accessed | tf_op | source)
XLA Modules:
  0.0 94.4 jit_solution(687543700214021410)
XLA Ops:
  0.7 0.0 copy-start.1
  0.7 0.8 kernel_pack.1
  1.5 16.4 %all_to_all.20.atoms_ref = f32[16,8,128]{2,1,0:T(8,128)S(1)} all-to-all(f32[16,8,128]{2,1,0:T(8,128)S(1)} %get-tuple-element.11), channel_id=1, replica_groups=mesh['grp'=16,'pme'=64] {'grp'}, dimensions={0} | all-to-all | bytes 131072 | tf_op jit(solution)/shard_map/all_to_all | solution.py:374
  17.8 0.0 copy-done.1
  17.9 1.7 %kernel_spread.1 = (bf16[64,2,384]{2,1,0:T(2,128)(2,1)S(1)}, bf16[256,2048]{1,0:T(8,128)(2,1)S(1)}, f32[4,8,2048]{2,1,0:T(8,128)S(1)}) custom-call(f32[16,8,128]{2,1,0:T(8,128)S(1)} %all_to_all.20.atoms_ref, bf16[512,512]{1,0:T(8,128)(2,1)S(1)} %copy-done.1), custom_call_target="tpu_custom_call" | custom-call | flops 1073741824 | bytes 1048576 | tf_op jit(solution)/shard_map/kernel_spread/pallas_call | solution.py:338
  19.5 0.0 copy-start
  19.5 0.0 copy-start.2
  19.6 0.0 copy-start.3
  19.6 0.0 copy-start.4
  19.6 40.8 %all_to_all.21.mesh_ref = bf16[64,2,384]{2,1,0:T(2,128)(2,1)S(1)} all-to-all(bf16[64,2,384]{2,1,0:T(2,128)(2,1)S(1)} %get-tuple-element.12), channel_id=1, replica_groups=mesh['grp'=16,'pme'=64] {'pme'}, dimensions={0} | all-to-all | bytes 196608 | tf_op jit(solution)/shard_map/all_to_all | solution.py:376
  60.4 0.0 copy-done
  60.4 0.0 copy-done.2
  60.4 0.0 copy-done.3
  60.4 0.0 copy-done.4
  60.4 0.7 kernel_waves.1
  61.2 21.0 %all_to_all.22.mesh_ref = bf16[64,2,384]{2,1,0:T(2,128)(2,1)S(1)} all-to-all(bf16[64,2,384]{2,1,0:T(2,128)(2,1)S(1)} %kernel_waves.1), channel_id=1, replica_groups=mesh['grp'=16,'pme'=64] {'pme'}, dimensions={0} | all-to-all | bytes 196608 | tf_op jit(solution)/shard_map/all_to_all | solution.py:377
  82.2 1.4 %kernel_sample.1 = f32[16,4,128]{2,1,0:T(4,128)S(1)} custom-call(f32[16,8,128]{2,1,0:T(8,128)S(1)} %all_to_all.20.atoms_ref, bf16[64,2,384]{2,1,0:T(2,128)(2,1)S(1)} %all_to_all.22.mesh_ref, bf16[512,512]{1,0:T(8,128)(2,1)S(1)} %copy-done.1, bf16[256,2048]{1,0:T(8,128)(2,1)S(1)} %get-tuple-element.13.y_ref, f32[4,8,2048]{2,1,0:T(8,128)S(1)} %get-tuple-element.14.x_ref), custom_call_target="tpu_custom_call" | custom-call | flops 1073741824 | bytes 1048576 | tf_op jit(solution)/shard_map/kernel_sample/pallas_call | solution.py:363
  83.6 10.2 %all_to_all.23.terms_ref = f32[16,4,128]{2,1,0:T(4,128)S(1)} all-to-all(f32[16,4,128]{2,1,0:T(4,128)S(1)} %kernel_sample.1), channel_id=1, replica_groups=mesh['grp'=16,'pme'=64] {'grp'}, dimensions={0} | all-to-all | bytes 65536 | tf_op jit(solution)/shard_map/all_to_all | solution.py:378
  93.8 0.6 kernel_total.1
Async XLA Ops:
  0.7 17.2 %copy-start.1 = (bf16[512,512]{1,0:T(8,128)(2,1)S(1)}, bf16[512,512]{1,0:T(8,128)(2,1)}, u32[]{:S(2)}) copy-start(bf16[512,512]{1,0:T(8,128)(2,1)} %constant.8.clone.table_ref) | copy-start | bytes 1572868
  19.5 40.9 %copy-start = (f32[8,4,512]{2,1,0:T(4,128)S(1)}, f32[8,4,512]{2,1,0:T(4,128)}, u32[]{:S(2)}) copy-start(f32[8,4,512]{2,1,0:T(4,128)} %green_ref.1) | copy-start | bytes 196612
  19.5 40.9 %copy-start.2 = (bf16[128,256]{1,0:T(8,128)(2,1)S(1)}, bf16[128,256]{1,0:T(8,128)(2,1)}, u32[]{:S(2)}) copy-start(bf16[128,256]{1,0:T(8,128)(2,1)} %constant.9.clone.table_ref) | copy-start | bytes 196612
  19.6 40.9 %copy-start.3 = (f32[16,512]{1,0:T(8,128)S(1)}, f32[16,512]{1,0:T(8,128)}, u32[]{:S(2)}) copy-start(f32[16,512]{1,0:T(8,128)} %constant.11.clone.sin_ref) | copy-start | bytes 98308
  19.6 40.8 %copy-start.4 = (f32[16,512]{1,0:T(8,128)S(1)}, f32[16,512]{1,0:T(8,128)}, u32[]{:S(2)}) copy-start(f32[16,512]{1,0:T(8,128)} %constant.10.clone.cos_ref) | copy-start | bytes 98308

commit v5 on v4

--- a/solution.py
+++ b/solution.py
@@ -166,15 +166,17 @@
 
 
 def own_waves(atoms_ref):
-    return whole(atoms_ref[0, 7:8, :]) * KX + lax.broadcasted_iota(jnp.int32, (KX, ATOMS), 0)
-
-
-def kernel_spread(atoms_ref, table_ref, out_ref, y_ref, x_ref, lead_ref):
+    return whole(atoms_ref[7, 0:1, :]) * KX + lax.broadcasted_iota(jnp.int32, (KX, ATOMS), 0)
+
+
+def kernel_spread(sent_ref, table_ref, out_ref, y_ref, x_ref, atoms_ref, lead_ref):
+    for k in range(8):
+        atoms_ref[k] = sent_ref[:, k, :]
     kx = own_waves(atoms_ref)
     steps = x_steps(kx)
-    charge = atoms_ref[:, 0, :]
-    wx, wy, wz = (spline(atoms_ref[:, 1 + d, :]) for d in range(3))
-    bx, by, bz = (whole(atoms_ref[:, 4 + d, :]) for d in range(3))
+    charge = atoms_ref[0]
+    wx, wy, wz = (spline(atoms_ref[1 + d]) for d in range(3))
+    bx, by, bz = (whole(atoms_ref[4 + d]) for d in range(3))
     ys = y_spots(by)
     z_at = lax.broadcasted_iota(jnp.int32, (16, ATOMS), 0)
     wz = [charge * w for w in wz]
@@ -245,9 +247,9 @@
 def kernel_sample(atoms_ref, mesh_ref, table_ref, y_ref, x_ref, out_ref, slope_ref):
     kx = own_waves(atoms_ref)
     steps = x_steps(kx)
-    wz = spline(atoms_ref[:, 3, :])
-    dx, dy, dz = (spline_slopes(atoms_ref[:, 1 + d, :]) for d in range(3))
-    by, bz = (whole(atoms_ref[:, 4 + d, :]) for d in range(1, 3))
+    wz = spline(atoms_ref[3])
+    dx, dy, dz = (spline_slopes(atoms_ref[1 + d]) for d in range(3))
+    by, bz = (whole(atoms_ref[4 + d]) for d in range(1, 3))
     ys = y_spots(by)
     z_at = lax.broadcasted_iota(jnp.int32, (16, ATOMS), 0)
     waves = mesh_ref[...].reshape(2 * SLABS, KY * SPAN).T
@@ -341,9 +343,10 @@
             jax.ShapeDtypeStruct(SENT, bf16),
             jax.ShapeDtypeStruct((NY, GROUPS * ATOMS), bf16),
             jax.ShapeDtypeStruct((4, KX, GROUPS * ATOMS), f32),
+            jax.ShapeDtypeStruct((8, GROUPS, ATOMS), f32),
         ],
         in_specs=[VMEM] * 2,
-        out_specs=[VMEM] * 3,
+        out_specs=[VMEM] * 4,
         scratch_shapes=[pltpu.VMEM((2 * LANES, GROUPS * ATOMS), bf16)],
         name="kernel_spread",
         compiler_params=pltpu.CompilerParams(vmem_limit_bytes=8 << 20),
@@ -372,7 +375,7 @@
     swap = functools.partial(lax.all_to_all, split_axis=0, concat_axis=0, tiled=True)
     packed, factors = pack(counts, charge, frac, base)
     atoms = swap(packed, "grp")
-    mesh, y_weights, x_sums = spread(atoms)
+    mesh, y_weights, x_sums, atoms = spread(atoms)
     mesh = swap(mesh, "pme")
     mesh = swap(wave_product(mesh, green), "pme")
     terms = swap(sample(atoms, mesh, y_weights, x_sums), "grp")

time: 94.7 us -> 94.5 us (level)
  no operation moved by 1% of the time
where the time goes in v5:
time: 94.5 us; the launch traced here: 94.2 us
  blocking collectives  88.4 us (94%)
  Pallas kernels  5.02 us (5%)
    all_to_all x1, blocking collectives, body(): mesh = swap(mesh, 'pme')  40.8 us
    all_to_all x1, blocking collectives, body(): mesh = swap(wave_product(mesh, green), 'pme')  21 us
    all_to_all x1, blocking collectives, body(): atoms = swap(packed, 'grp')  16.4 us
    all_to_all x1, blocking collectives, body(): terms = swap(sample(atoms, mesh, y_weights, x_sums), 'grp')  10.2 us

profile of v5, /device:TPU:1, one launch (start us, length us, event | category | flops | bytes accessed | tf_op | source)
XLA Modules:
  0.0 94.2 jit_solution(16641278276664914468)
XLA Ops:
  0.7 0.0 copy-start.1
  0.7 0.8 kernel_pack.1
  1.5 16.4 %all_to_all.20.sent_ref = f32[16,8,128]{2,1,0:T(8,128)S(1)} all-to-all(f32[16,8,128]{2,1,0:T(8,128)S(1)} %get-tuple-element.12), channel_id=1, replica_groups=mesh['grp'=16,'pme'=64] {'grp'}, dimensions={0} | all-to-all | bytes 131072 | tf_op jit(solution)/shard_map/all_to_all | solution.py:377
  17.8 0.0 copy-done.1
  17.9 1.6 %kernel_spread.1 = (bf16[64,2,384]{2,1,0:T(2,128)(2,1)S(1)}, bf16[256,2048]{1,0:T(8,128)(2,1)S(1)}, f32[4,8,2048]{2,1,0:T(8,128)S(1)}, f32[8,16,128]{2,1,0:T(8,128)S(1)}) custom-call(f32[16,8,128]{2,1,0:T(8,128)S(1)} %all_to_all.20.sent_ref, bf16[512,512]{1,0:T(8,128)(2,1)S(1)} %copy-done.1), custom_call_target="tpu_custom_call" | custom-call | flops 1073741824 | bytes 1048576 | tf_op jit(solution)/shard_map/kernel_spread/pallas_call | solution.py:340
  19.4 0.0 copy-start
  19.5 0.0 copy-start.2
  19.5 0.0 copy-start.3
  19.5 0.0 copy-start.4
  19.5 40.8 %all_to_all.21.mesh_ref = bf16[64,2,384]{2,1,0:T(2,128)(2,1)S(1)} all-to-all(bf16[64,2,384]{2,1,0:T(2,128)(2,1)S(1)} %get-tuple-element.14), channel_id=1, replica_groups=mesh['grp'=16,'pme'=64] {'pme'}, dimensions={0} | all-to-all | bytes 196608 | tf_op jit(solution)/shard_map/all_to_all | solution.py:379
  60.3 0.0 copy-done
  60.3 0.0 copy-done.2
  60.3 0.0 copy-done.3
  60.3 0.0 copy-done.4
  60.3 0.7 kernel_waves.1
  61.1 21.0 %all_to_all.22.mesh_ref = bf16[64,2,384]{2,1,0:T(2,128)(2,1)S(1)} all-to-all(bf16[64,2,384]{2,1,0:T(2,128)(2,1)S(1)} %kernel_waves.1), channel_id=1, replica_groups=mesh['grp'=16,'pme'=64] {'pme'}, dimensions={0} | all-to-all | bytes 196608 | tf_op jit(solution)/shard_map/all_to_all | solution.py:380
  82.1 1.3 %kernel_sample.1 = f32[16,4,128]{2,1,0:T(4,128)S(1)} custom-call(f32[8,16,128]{2,1,0:T(8,128)S(1)} %get-tuple-element.13.atoms_ref, bf16[64,2,384]{2,1,0:T(2,128)(2,1)S(1)} %all_to_all.22.mesh_ref, bf16[512,512]{1,0:T(8,128)(2,1)S(1)} %copy-done.1, bf16[256,2048]{1,0:T(8,128)(2,1)S(1)} %get-tuple-element.15.y_ref, f32[4,8,2048]{2,1,0:T(8,128)S(1)} %get-tuple-element.16.x_ref), custom_call_target="tpu_custom_call" | custom-call | flops 1073741824 | bytes 1048576 | tf_op jit(solution)/shard_map/kernel_sample/pallas_call | solution.py:366
  83.4 10.2 %all_to_all.23.terms_ref = f32[16,4,128]{2,1,0:T(4,128)S(1)} all-to-all(f32[16,4,128]{2,1,0:T(4,128)S(1)} %kernel_sample.1), channel_id=1, replica_groups=mesh['grp'=16,'pme'=64] {'grp'}, dimensions={0} | all-to-all | bytes 65536 | tf_op jit(solution)/shard_map/all_to_all | solution.py:381
  93.6 0.6 kernel_total.1
Async XLA Ops:
  0.7 17.2 %copy-start.1 = (bf16[512,512]{1,0:T(8,128)(2,1)S(1)}, bf16[512,512]{1,0:T(8,128)(2,1)}, u32[]{:S(2)}) copy-start(bf16[512,512]{1,0:T(8,128)(2,1)} %constant.8.clone.table_ref) | copy-start | bytes 1572868
  19.4 40.9 %copy-start = (f32[8,4,512]{2,1,0:T(4,128)S(1)}, f32[8,4,512]{2,1,0:T(4,128)}, u32[]{:S(2)}) copy-start(f32[8,4,512]{2,1,0:T(4,128)} %green_ref.1) | copy-start | bytes 196612
  19.5 40.9 %copy-start.2 = (bf16[128,256]{1,0:T(8,128)(2,1)S(1)}, bf16[128,256]{1,0:T(8,128)(2,1)}, u32[]{:S(2)}) copy-start(bf16[128,256]{1,0:T(8,128)(2,1)} %constant.9.clone.table_ref) | copy-start | bytes 196612
  19.5 40.9 %copy-start.3 = (f32[16,512]{1,0:T(8,128)S(1)}, f32[16,512]{1,0:T(8,128)}, u32[]{:S(2)}) copy-start(f32[16,512]{1,0:T(8,128)} %constant.11.clone.sin_ref) | copy-start | bytes 98308
  19.5 40.8 %copy-start.4 = (f32[16,512]{1,0:T(8,128)S(1)}, f32[16,512]{1,0:T(8,128)}, u32[]{:S(2)}) copy-start(f32[16,512]{1,0:T(8,128)} %constant.10.clone.cos_ref) | copy-start | bytes 98308

commit v6 on v5

--- a/solution.py
+++ b/solution.py
@@ -295,13 +295,6 @@
             sample_block(g - 1 + h, level[:, at], slope[:, at])
 
 
-def kernel_total(factor_ref, terms_ref, out_ref):
-    total = terms_ref[0]
-    for g in range(1, GROUPS):
-        total = total + terms_ref[g]
-    out_ref[...] = total * factor_ref[...]
-
-
 def call(kernel, shape, dtype, inputs, scratch=(), flops=0, limit=8):
     return pl.pallas_call(
         kernel,
@@ -367,7 +360,7 @@
 
 
 def total(factors, terms):
-    return call(kernel_total, (4, ATOMS), f32, 2)(factors, terms)
+    return jnp.sum(terms, axis=0) * factors
 
 
 def body(charge, base, frac, counts, green):

time: 94.5 us -> 94.5 us (level)
  no operation moved by 1% of the time
where the time goes in v6:
time: 94.5 us; the launch traced here: 94.2 us
  blocking collectives  88.4 us (94%)
  Pallas kernels  4.4 us (5%)
    all_to_all x1, blocking collectives, body(): mesh = swap(mesh, 'pme')  40.8 us
    all_to_all x1, blocking collectives, body(): mesh = swap(wave_product(mesh, green), 'pme')  21 us
    all_to_all x1, blocking collectives, body(): atoms = swap(packed, 'grp')  16.4 us
    all_to_all x1, blocking collectives, body(): terms = swap(sample(atoms, mesh, y_weights, x_sums), 'grp')  10.2 us

profile of v6, /device:TPU:1, one launch (start us, length us, event | category | flops | bytes accessed | tf_op | source)
XLA Modules:
  0.0 94.2 jit_solution(16687549137069439647)
XLA Ops:
  0.7 0.0 copy-start.1
  0.7 0.8 kernel_pack.1
  1.5 16.4 %all_to_all.20.sent_ref = f32[16,8,128]{2,1,0:T(8,128)S(1)} all-to-all(f32[16,8,128]{2,1,0:T(8,128)S(1)} %get-tuple-element.11), channel_id=1, replica_groups=mesh['grp'=16,'pme'=64] {'grp'}, dimensions={0} | all-to-all | bytes 131072 | tf_op jit(solution)/shard_map/all_to_all | solution.py:370
  17.8 0.0 copy-done.1
  17.9 1.5 %kernel_spread.1 = (bf16[64,2,384]{2,1,0:T(2,128)(2,1)S(1)}, bf16[256,2048]{1,0:T(8,128)(2,1)S(1)}, f32[4,8,2048]{2,1,0:T(8,128)S(1)}, f32[8,16,128]{2,1,0:T(8,128)S(1)}) custom-call(f32[16,8,128]{2,1,0:T(8,128)S(1)} %all_to_all.20.sent_ref, bf16[512,512]{1,0:T(8,128)(2,1)S(1)} %copy-done.1), custom_call_target="tpu_custom_call" | custom-call | flops 1073741824 | bytes 1048576 | tf_op jit(solution)/shard_map/kernel_spread/pallas_call | solution.py:333
  19.4 0.0 copy-start
  19.4 0.0 copy-start.2
  19.4 0.0 copy-start.3
  19.4 0.0 copy-start.4
  19.5 40.8 %all_to_all.21.mesh_ref = bf16[64,2,384]{2,1,0:T(2,128)(2,1)S(1)} all-to-all(bf16[64,2,384]{2,1,0:T(2,128)(2,1)S(1)} %get-tuple-element.13), channel_id=1, replica_groups=mesh['grp'=16,'pme'=64] {'pme'}, dimensions={0} | all-to-all | bytes 196608 | tf_op jit(solution)/shard_map/all_to_all | solution.py:372
  60.3 0.0 copy-done
  60.3 0.0 copy-done.2
  60.3 0.0 copy-done.3
  60.3 0.0 copy-done.4
  60.3 0.7 kernel_waves.1
  61.1 21.0 %all_to_all.22.mesh_ref = bf16[64,2,384]{2,1,0:T(2,128)(2,1)S(1)} all-to-all(bf16[64,2,384]{2,1,0:T(2,128)(2,1)S(1)} %kernel_waves.1), channel_id=1, replica_groups=mesh['grp'=16,'pme'=64] {'pme'}, dimensions={0} | all-to-all | bytes 196608 | tf_op jit(solution)/shard_map/all_to_all | solution.py:373
  82.1 1.3 %kernel_sample.1 = f32[16,4,128]{2,1,0:T(4,128)S(1)} custom-call(f32[8,16,128]{2,1,0:T(8,128)S(1)} %get-tuple-element.12.atoms_ref, bf16[64,2,384]{2,1,0:T(2,128)(2,1)S(1)} %all_to_all.22.mesh_ref, bf16[512,512]{1,0:T(8,128)(2,1)S(1)} %copy-done.1, bf16[256,2048]{1,0:T(8,128)(2,1)S(1)} %get-tuple-element.14.y_ref, f32[4,8,2048]{2,1,0:T(8,128)S(1)} %get-tuple-element.15.x_ref), custom_call_target="tpu_custom_call" | custom-call | flops 1073741824 | bytes 1048576 | tf_op jit(solution)/shard_map/kernel_sample/pallas_call | solution.py:359
  83.4 10.2 %all_to_all.23 = f32[16,4,128]{2,1,0:T(4,128)S(1)} all-to-all(f32[16,4,128]{2,1,0:T(4,128)S(1)} %kernel_sample.1), channel_id=1, replica_groups=mesh['grp'=16,'pme'=64] {'grp'}, dimensions={0} | all-to-all | bytes 65536 | tf_op jit(solution)/shard_map/all_to_all | solution.py:374
  93.6 0.6 mul.3
  (1 shorter events, 0.0 us)
Async XLA Ops:
  0.7 17.2 %copy-start.1 = (bf16[512,512]{1,0:T(8,128)(2,1)S(1)}, bf16[512,512]{1,0:T(8,128)(2,1)}, u32[]{:S(2)}) copy-start(bf16[512,512]{1,0:T(8,128)(2,1)} %constant.10.clone.table_ref) | copy-start | bytes 1572868
  19.4 40.9 %copy-start = (f32[8,4,512]{2,1,0:T(4,128)S(1)}, f32[8,4,512]{2,1,0:T(4,128)}, u32[]{:S(2)}) copy-start(f32[8,4,512]{2,1,0:T(4,128)} %green_ref.1) | copy-start | bytes 196612
  19.4 40.9 %copy-start.2 = (bf16[128,256]{1,0:T(8,128)(2,1)S(1)}, bf16[128,256]{1,0:T(8,128)(2,1)}, u32[]{:S(2)}) copy-start(bf16[128,256]{1,0:T(8,128)(2,1)} %constant.11.clone.table_ref) | copy-start | bytes 196612
  19.4 40.9 %copy-start.3 = (f32[16,512]{1,0:T(8,128)S(1)}, f32[16,512]{1,0:T(8,128)}, u32[]{:S(2)}) copy-start(f32[16,512]{1,0:T(8,128)} %constant.13.clone.sin_ref) | copy-start | bytes 98308
  19.4 40.8 %copy-start.4 = (f32[16,512]{1,0:T(8,128)S(1)}, f32[16,512]{1,0:T(8,128)}, u32[]{:S(2)}) copy-start(f32[16,512]{1,0:T(8,128)} %constant.12.clone.cos_ref) | copy-start | bytes 98308
